TPU v7x, 32 devices: a whole 2x2x4 slice. The times are simulated.
32 devices in a mesh: sub: 16 (over z, y, core), tm: 2 (over x).
Axes of the slice: x: 2, y: 2, z: 4, core: 2. Of those that a mesh axis runs over, the one named last changes fastest.
Arguments:
- voltages: bfloat16 [192, 2, 96, 2048], P('sub', None, None, 'tm'), may hold values from -6 to 6
- pointing_table: bfloat16 [192, 2, 320, 96], P('sub'), may hold values from -0.4375 to 0.4375
- beam_pointing: int32 [256], replicated, may hold values from 0 to 319
- subband_order: int32 [192], replicated, may hold values from 0 to 191, each once
- live_subbands: int32 [1], replicated, may hold values from 152 to 192
- filter_taps: float32 [16, 16], replicated, may hold values from -0.36 to 0.36
Outputs:
- synthesised: bfloat16 [256, 12, 2, 32768], P('sub', None, None, 'tm')
Inputs may be any that keep to these rules, and one draw needn't show every extreme that they name: `subband_order`: each slot is named by exactly one frequency.
All inputs are finite; a program needn't handle non-finite values.
Results may differ from a plain program's by a relative error of at most 0.0052.
Values may be sent and summed in bfloat16 or wider, within the bound.
No kernel may reach another device: no remote copies, remote signals or barrier semaphores. Data moves between devices by JAX's collectives and lax.ppermute only.
A program may use at most 192 MiB of HBM per device.

v0:
```python
import math
import jax
import jax.numpy as jnp
from jax import lax
from jax.sharding import PartitionSpec as P


def shifted(block, axis, distance):
    devices = range(lax.axis_size(axis))
    route = [(i - distance, i) for i in devices if i - distance in devices]
    return lax.ppermute(block, axis, route)


def inverse_table(channel_count):
    channel_index = jnp.arange(channel_count, dtype=jnp.int32)
    phase = (jnp.outer(channel_index, channel_index) % channel_count).astype(jnp.float32) * (
        2.0 * math.pi / channel_count
    )
    cosine = jnp.cos(phase).astype(jnp.bfloat16)
    sine_table = jnp.sin(phase).astype(jnp.bfloat16)
    upper_rows = jnp.stack([cosine, -sine_table], axis=1)
    lower_rows = jnp.stack([sine_table, cosine], axis=1)
    return jnp.stack([upper_rows, lower_rows], axis=0)


def spectrum_channels(beam_rows, subband_order, live_subbands, inverse_rows):
    slot_count = beam_rows.shape[0]
    channel_count = inverse_rows.shape[1]
    spectrum = jnp.take(beam_rows, subband_order, axis=0)
    live_mask = jnp.arange(slot_count, dtype=jnp.int32) < live_subbands[0]
    spectrum = jnp.where(live_mask[:, None, None, None], spectrum, jnp.zeros_like(spectrum))
    grouped = spectrum.reshape(
        slot_count // channel_count, channel_count, beam_rows.shape[1], 2, beam_rows.shape[3]
    )
    channels = jnp.einsum(
        "qkpc,gcbpt->bgqkt", inverse_rows, grouped, preferred_element_type=jnp.float32
    )
    return (grouped, channels)


def polyphase(channels, earlier, filter_taps):
    length = channels.shape[4]
    tap_count = filter_taps.shape[0]
    extended = jnp.concatenate([earlier, channels], axis=4)
    running = jnp.zeros_like(channels)
    for tap_index in range(tap_count):
        offset = tap_count - 1 - tap_index
        running = (
            running + filter_taps[tap_index][:, None] * extended[..., offset : offset + length]
        )
    channel_shape = channels.shape
    return (
        jnp.swapaxes(running, 3, 4)
        .reshape(channel_shape[0], channel_shape[1], 2, length * channel_shape[3])
        .astype(jnp.bfloat16)
    )


def on_device(voltages, pointing_table, beam_pointing, subband_order, live_subbands, filter_taps):
    local_subbands = voltages.shape[0]
    inputs = voltages.shape[2]
    local_time = voltages.shape[3]
    beam_count = beam_pointing.shape[0]
    rim_width = filter_taps.shape[0] - 1
    chosen = jnp.take(pointing_table, beam_pointing, axis=2)
    real_weight = chosen[:, 0]
    imag_weight = chosen[:, 1]
    stacked = jnp.stack(
        [
            jnp.concatenate([real_weight, -imag_weight], axis=2),
            jnp.concatenate([imag_weight, real_weight], axis=2),
        ],
        axis=2,
    )
    stacked = stacked.reshape(local_subbands, 2 * beam_count, 2 * inputs)
    signal = voltages.reshape(local_subbands, 2 * inputs, local_time)
    formed = jnp.einsum("sqi,sit->sqt", stacked, signal, preferred_element_type=jnp.float32).astype(
        jnp.bfloat16
    )
    inverse_rows = inverse_table(filter_taps.shape[1])
    axis_devices = lax.axis_size("sub")
    beam_part = beam_count // axis_devices
    blocks = formed.reshape(local_subbands, axis_devices, beam_part, 2, local_time)
    beam_rows = lax.all_to_all(blocks, "sub", split_axis=1, concat_axis=0, tiled=True)[:, 0]
    grouped, channels = spectrum_channels(beam_rows, subband_order, live_subbands, inverse_rows)
    earlier = shifted(channels[..., local_time - rim_width :].astype(jnp.bfloat16), "tm", 1).astype(
        jnp.float32
    )
    return polyphase(channels, earlier, filter_taps)


def solution(mesh):
    in_specs = (P("sub", None, None, "tm"), P("sub", None, None, None), P(), P(), P(), P())
    out_specs = P("sub", None, None, "tm")
    return jax.shard_map(
        on_device, mesh=mesh, in_specs=in_specs, out_specs=out_specs, check_vma=False
    )
```

profile of v0, /device:TPU:14, one launch (start us, length us, event | category | flops | bytes accessed | tf_op | source)
XLA Modules:
  0.0 792.8 jit_solution(15740473894358660357)
XLA Ops:
  0.0 0.7 compare_and_fusion
  0.7 0.7 compare_select_fusion
  1.4 5.8 copy.47
  7.1 5.2 gather_fusion
  12.4 2.1 fusion.51
  14.5 2.2 fusion.62
  16.7 2.8 copy.49
  19.5 1.1 bitcast_negate_fusion
  20.6 1.3 copy.48
  21.9 1.3 maximum_bitcast_fusion
  23.2 0.2 pad_maximum_fusion.1
  23.4 5.5 copy.50
  28.9 5.2 reshape.129
  34.1 8.9 %convolution_convert_fusion = bf16[12,512,1024]{2,1,0:T(8,128)(2,1)} fusion(bf16[12,512,192]{2,1,0:T(8,128)(2,1)S(1)} %reshape.129, bf16[12,192,1024]{2,1,0:T(8,128)(2,1)} %bitcast.74), kind=kOutput, calls=%fused_computation.81 | convolution fusion | flops 2422210560 | bytes 19660800 | tf_op jit(solution)/shard_map/sqi,sit->sqt/dot_general | solution.py:77
  43.1 19.0 %reshape.131 = bf16[12,16,16,2,1024]{4,3,2,1,0:T(2,128)(2,1)} reshape(bf16[12,512,1024]{2,1,0:T(8,128)(2,1)} %convolution_convert_fusion) | data formatting | bytes 25165824 | tf_op jit(solution)/shard_map/reshape | solution.py:83
  62.1 0.0 copy-start.1
  62.1 12.5 %copy.52 = bf16[12,16,16,2,1024]{4,2,3,0,1:T(8,128)(2,1)} copy(bf16[12,16,16,2,1024]{4,3,2,1,0:T(2,128)(2,1)} %reshape.131) | data formatting | bytes 25165824 | tf_op jit(solution)/shard_map/reshape | solution.py:83
  74.6 6.2 all-to-all-start
  81.5 0.0 copy-done.1
  81.5 0.1 broadcast_in_dim.41
  81.6 0.1 fusion.60
  81.7 0.1 sine_convert_fusion
  81.8 271.0 %all-to-all-done = bf16[12,16,16,2,1024]{4,2,3,0,1:T(8,128)(2,1)} async-done(((bf16[12,16,16,2,1024]{4,2,3,0,1:T(8,128)(2,1)}), bf16[12,16,16,2,1024]{4,2,3,0,1:T(8,128)(2,1)}, u32[]{:S(2)}, u32[]{:S(2)}) %all-to-all-start) | async-done | bytes 12582944 | tf_op jit(solution)/shard_map/all_to_all | solution.py:84
  352.8 12.8 %gather_fusion.1 = bf16[192,16,2,1024]{3,1,2,0:T(8,128)(2,1)} fusion(bf16[192,16,2,1024]{3,1,2,0:T(8,128)(2,1)} %bitcast.10, s32[1024]{0:T(1024)S(1)} %pad_clamp_fusion), kind=kCustom, calls=%fused_computation.1 | custom fusion | bytes 25166592 | tf_op jit(solution)/shard_map/jit(_take)/gather | solution.py:29
  365.6 6.8 select_bitcast_fusion
  372.4 0.0 copy-start
  372.4 12.4 %fusion.48 = f32[16,12,2,16,1024]{4,3,2,0,1:T(8,128)} fusion(bf16[12,16,16,2,1024,1]{4,2,3,1,0,5:T(8,128)(2,1)S(1)} %select_bitcast_fusion, bf16[1,16,2,16]{3,1,2,0:T(8,128)(2,1)S(1)} %get-tuple-element.26, bf16[1,16,2,16]{3,1,2,0:T(8,128)(2,1)S(1)} %get-tuple-element.25), kind=kOutput, calls=%fused_computation.80 | convolution fusion | flops 402657280 | bytes 37750784 | tf_op jit(solution)/shard_map/qkpc,gcbpt->bgqkt/dot_general | solution.py:35
  384.8 2.4 slice.415
  387.2 3.1 copy.54
  390.3 1.5 collective-permute-start
  391.8 0.0 copy-done
  391.8 35.0 %collective-permute-done = bf16[16,12,2,16,15]{3,0,4,2,1:T(8,128)(2,1)} collective-permute-done((bf16[16,12,2,16,15]{3,0,4,2,1:T(8,128)(2,1)S(1)}, bf16[16,12,2,16,15]{3,0,4,2,1:T(8,128)(2,1)}, u32[]{:S(2)}, u32[]{:S(2)}) %collective-permute-start) | collective-permute-done | bytes 184352 | tf_op jit(solution)/shard_map/ppermute | solution.py:11
  426.9 3.5 copy.55
  430.4 168.7 %fusion.47 = bf16[16,12,2,1024,16]{3,4,2,0,1:T(8,128)(2,1)} fusion(f32[16,12,2,16,1024]{4,3,2,0,1:T(8,128)} %fusion.48, f32[16,12,2,16,15]{4,3,2,0,1:T(8,128)S(1)} %copy.55, f32[16]{0:T(128)S(1)} %get-tuple-element.23, f32[16]{0:T(128)S(1)} %get-tuple-element.24, f32[16]{0:T(128)S(1)} %get-tuple-element.10, f32[16]{0:T(128)S(1)} %get-tuple-element.11, ...), kind=kLoop, calls=%fused_computation.79 | loop fusion | flops 295698432 | bytes 38118400 | tf_op jit(solution)/shard_map/convert_element_type | solution.py:55
  599.1 77.5 %copy.64 = bf16[16,12,2,1024,16]{4,3,2,1,0:T(8,128)(2,1)} copy(bf16[16,12,2,1024,16]{3,4,2,0,1:T(8,128)(2,1)} %fusion.47) | data formatting | bytes 25165824 | tf_op jit(solution)/shard_map/convert_element_type | solution.py:55
  676.7 116.1 %reshape.153 = bf16[16,12,2,16384]{3,2,1,0:T(2,128)(2,1)} reshape(bf16[16,12,2,1024,16]{4,3,2,1,0:T(8,128)(2,1)} %copy.64) | data formatting | bytes 25165824 | tf_op jit(solution)/shard_map/convert_element_type | solution.py:55
  (7 shorter events, 0.1 us)
Async XLA Ops:
  62.1 19.4 %copy-start.1 = (s32[192]{0:T(256)S(1)}, s32[192]{0:T(256)}, u32[]{:S(2)}) copy-start(s32[192]{0:T(256)} %param.9) | copy-start | bytes 2308
  74.6 278.2 %all-to-all-start = ((bf16[12,16,16,2,1024]{4,2,3,0,1:T(8,128)(2,1)}), bf16[12,16,16,2,1024]{4,2,3,0,1:T(8,128)(2,1)}, u32[]{:S(2)}, u32[]{:S(2)}) async-start(bf16[12,16,16,2,1024]{4,2,3,0,1:T(8,128)(2,1)} %copy.52), calls=%async_computation | async-start | bytes 25165824 | tf_op jit(solution)/shard_map/all_to_all | solution.py:84
  372.4 19.4 %copy-start = (f32[16,16]{1,0:T(8,128)S(1)}, f32[16,16]{1,0:T(8,128)}, u32[]{:S(2)}) copy-start(f32[16,16]{1,0:T(8,128)} %param.11) | copy-start | bytes 3076
  390.3 36.6 %collective-permute-start = (bf16[16,12,2,16,15]{3,0,4,2,1:T(8,128)(2,1)S(1)}, bf16[16,12,2,16,15]{3,0,4,2,1:T(8,128)(2,1)}, u32[]{:S(2)}, u32[]{:S(2)}) collective-permute-start(bf16[16,12,2,16,15]{3,0,4,2,1:T(8,128)(2,1)S(1)} %copy.54), channel_id=1, source_target_pairs={{0,1},{2,3},{4,5},{6,7},{8,9},{10,11},{12,13},{14,15},{16,17},{18,... | collective-permute-start | bytes 552968 | tf_op jit(solution)/shard_map/ppermute | solution.py:11
where the time goes:
time: 799 us; the launch traced here: 793 us
  waiting for transfers between devices  306 us (38%)
  local copies, waits for them, and re-layouts  275 us (34%)
  other arithmetic  182 us (23%)
  matrix products  21.3 us (3%)
    all_to_all x1, waiting for transfers between devices, on_device(): lax.all_to_all(blocks, 'sub', split_axis=1, concat_axis=0, tiled=True)[:, 0]  271 us
    convert_element_type x2, local copies, waits for them, and re-layouts, polyphase(): return jnp.swapaxes(running, 3, 4).reshape(channel_shape[0], channel_shap...  194 us
    convert_element_type x1, other arithmetic, polyphase(): return jnp.swapaxes(running, 3, 4).reshape(channel_shape[0], channel_shap...  169 us
    ppermute x1, waiting for transfers between devices, shifted(): return lax.ppermute(block, axis, route)  35 us
    reshape x2, local copies, waits for them, and re-layouts, on_device(): formed.reshape(local_subbands, axis_devices, beam_part, 2, local_time)  31.6 us
  transfers between devices with their start and end apart: 2, of which 2 were waited for; matrix products, arithmetic and copies ran while one was open for 0% of the time, Pallas kernels for 0%

commit v1 on v0

--- a/solution.py
+++ b/solution.py
@@ -81,7 +81,10 @@
     axis_devices = lax.axis_size("sub")
     beam_part = beam_count // axis_devices
     blocks = formed.reshape(local_subbands, axis_devices, beam_part, 2, local_time)
-    beam_rows = lax.all_to_all(blocks, "sub", split_axis=1, concat_axis=0, tiled=True)[:, 0]
+    beam_rows = jnp.concatenate(
+        lax.all_to_all(jnp.stack(jnp.split(blocks, lax.axis_size("sub"), axis=1)), "sub", 0, 0),
+        axis=0,
+    )[:, 0]
     grouped, channels = spectrum_channels(beam_rows, subband_order, live_subbands, inverse_rows)
     earlier = shifted(channels[..., local_time - rim_width :].astype(jnp.bfloat16), "tm", 1).astype(
         jnp.float32

time: 799 us -> 842 us (1.054)
  local copies, waits for them, and re-layouts: 275 us -> 318 us
    unnamed x5 -> x20, local copies, waits for them, and re-layouts: 5.77 us -> 45.8 us
    reshape x2 -> x1, local copies, waits for them, and re-layouts: 31.6 us -> 19 us  [on_device(): formed.reshape(local_subbands, axis_devices, beam_part, 2, local_time)]
    all_to_all x0 -> x1, local copies, waits for them, and re-layouts: none -> 12.5 us  [on_device(): lax.all_to_all(jnp.stack(jnp.split(blocks, lax.axis_size('sub'), axis=1))...]
where the time goes in v1:
time: 842 us; the launch traced here: 836 us
  local copies, waits for them, and re-layouts  318 us (38%)
  waiting for transfers between devices  306 us (36%)
  other arithmetic  182 us (22%)
  matrix products  21.3 us (3%)
    all_to_all x1, waiting for transfers between devices, on_device(): lax.all_to_all(jnp.stack(jnp.split(blocks, lax.axis_size('sub'), axis=1))...  271 us
    convert_element_type x2, local copies, waits for them, and re-layouts, polyphase(): return jnp.swapaxes(running, 3, 4).reshape(channel_shape[0], channel_shap...  194 us
    convert_element_type x1, other arithmetic, polyphase(): return jnp.swapaxes(running, 3, 4).reshape(channel_shape[0], channel_shap...  169 us
    unnamed x20, local copies, waits for them, and re-layouts  45.8 us
    ppermute x1, waiting for transfers between devices, shifted(): return lax.ppermute(block, axis, route)  35.3 us
    reshape x1, local copies, waits for them, and re-layouts, on_device(): formed.reshape(local_subbands, axis_devices, beam_part, 2, local_time)  19 us
  transfers between devices with their start and end apart: 2, of which 2 were waited for; matrix products, arithmetic and copies ran while one was open for 0% of the time, Pallas kernels for 0%

profile of v1, /device:TPU:14, one launch (start us, length us, event | category | flops | bytes accessed | tf_op | source)
XLA Modules:
  0.0 835.6 jit_solution(8149960359821808907)
XLA Ops:
  0.0 0.7 compare_and_fusion
  0.7 0.7 compare_select_fusion
  1.4 5.8 copy.121
  7.1 5.2 gather_fusion
  12.4 2.1 fusion.51
  14.5 2.2 fusion.78
  16.7 2.8 copy.123
  19.5 1.1 bitcast_negate_fusion
  20.6 1.3 copy.122
  21.9 1.3 maximum_bitcast_fusion
  23.2 0.2 pad_maximum_fusion.1
  23.4 5.5 copy.124
  28.9 5.2 reshape.128
  34.1 8.9 %convolution_convert_fusion = bf16[12,512,1024]{2,1,0:T(8,128)(2,1)} fusion(bf16[12,512,192]{2,1,0:T(8,128)(2,1)S(1)} %reshape.128, bf16[12,192,1024]{2,1,0:T(8,128)(2,1)} %bitcast.165), kind=kOutput, calls=%fused_computation.81 | convolution fusion | flops 2422210560 | bytes 19660800 | tf_op jit(solution)/shard_map/sqi,sit->sqt/dot_general | solution.py:77
  43.1 19.0 %reshape.130 = bf16[12,16,16,2,1024]{4,3,2,1,0:T(2,128)(2,1)} reshape(bf16[12,512,1024]{2,1,0:T(8,128)(2,1)} %convolution_convert_fusion) | data formatting | bytes 25165824 | tf_op jit(solution)/shard_map/reshape | solution.py:83
  62.1 2.7 fusion.67
  64.8 2.7 fusion.66
  67.4 2.7 fusion.65
  70.1 2.7 fusion.64
  72.8 2.7 fusion.63
  75.4 2.7 fusion.62
  78.1 2.7 fusion.61
  80.8 2.7 fusion.60
  83.5 2.7 fusion.59
  86.1 2.7 fusion.58
  88.8 2.7 fusion.57
  91.5 2.7 fusion.56
  94.1 2.7 fusion.55
  96.8 2.7 fusion.54
  99.5 2.7 fusion.53
  102.1 2.7 fusion.52
  104.8 6.4 all-to-all-start
  111.9 0.1 broadcast_in_dim.41
  112.0 0.1 fusion.76
  112.1 0.1 sine_convert_fusion
  112.1 271.0 %all-to-all-done = bf16[16,12,1,16,2,1024]{5,4,3,1,2,0:T(2,128)(2,1)} async-done(((bf16[16,12,1,16,2,1024]{5,4,3,1,2,0:T(2,128)(2,1)}), bf16[16,12,1,16,2,1024]{5,4,3,1,2,0:T(2,128)(2,1)}, u32[]{:S(2)}, u32[]{:S(2)}) %all-to-all-start) | async-done | bytes 12582944 | tf_op jit(solution)/shard_map/all_to_all | solution.py:85
  383.1 12.5 %copy.141 = bf16[16,12,1,16,2,1024]{5,3,4,1,0,2:T(8,128)(2,1)} copy(bf16[16,12,1,16,2,1024]{5,4,3,1,2,0:T(2,128)(2,1)} %all-to-all-done) | data formatting | bytes 25165824 | tf_op jit(solution)/shard_map/all_to_all | solution.py:85
  395.7 12.8 %gather_fusion.1 = bf16[192,16,2,1024]{3,1,2,0:T(8,128)(2,1)} fusion(bf16[192,16,2,1024]{3,1,2,0:T(8,128)(2,1)} %bitcast.162, s32[1024]{0:T(1024)S(1)} %pad_clamp_fusion), kind=kCustom, calls=%fused_computation.1 | custom fusion | bytes 25166592 | tf_op jit(solution)/shard_map/jit(_take)/gather | solution.py:29
  408.5 6.8 select_bitcast_fusion
  415.3 12.4 %fusion.48 = f32[16,12,2,16,1024]{4,3,2,0,1:T(8,128)} fusion(bf16[12,16,16,2,1024,1]{4,2,3,1,0,5:T(8,128)(2,1)S(1)} %select_bitcast_fusion, bf16[1,16,2,16]{3,1,2,0:T(8,128)(2,1)S(1)} %get-tuple-element.26, bf16[1,16,2,16]{3,1,2,0:T(8,128)(2,1)S(1)} %get-tuple-element.25), kind=kOutput, calls=%fused_computation.80 | convolution fusion | flops 402657280 | bytes 37750784 | tf_op jit(solution)/shard_map/qkpc,gcbpt->bgqkt/dot_general | solution.py:35
  427.6 2.4 slice.415
  430.0 3.1 copy.143
  433.1 1.3 collective-permute-start
  434.5 35.3 %collective-permute-done = bf16[16,12,2,16,15]{3,0,4,2,1:T(8,128)(2,1)} collective-permute-done((bf16[16,12,2,16,15]{3,0,4,2,1:T(8,128)(2,1)S(1)}, bf16[16,12,2,16,15]{3,0,4,2,1:T(8,128)(2,1)}, u32[]{:S(2)}, u32[]{:S(2)}) %collective-permute-start) | collective-permute-done | bytes 184352 | tf_op jit(solution)/shard_map/ppermute | solution.py:11
  469.7 3.5 copy.144
  473.3 168.7 %fusion.47 = bf16[16,12,2,1024,16]{3,4,2,0,1:T(8,128)(2,1)} fusion(f32[16,12,2,16,1024]{4,3,2,0,1:T(8,128)} %fusion.48, f32[16,12,2,16,15]{4,3,2,0,1:T(8,128)S(1)} %copy.144, f32[16]{0:T(128)S(1)} %get-tuple-element.23, f32[16]{0:T(128)S(1)} %get-tuple-element.24, f32[16]{0:T(128)S(1)} %get-tuple-element.10, f32[16]{0:T(128)S(1)} %get-tuple-element.11, ...), kind=kLoop, calls=%fused_computation.79 | loop fusion | flops 295698432 | bytes 38118400 | tf_op jit(solution)/shard_map/convert_element_type | solution.py:55
  642.0 77.5 %copy.153 = bf16[16,12,2,1024,16]{4,3,2,1,0:T(8,128)(2,1)} copy(bf16[16,12,2,1024,16]{3,4,2,0,1:T(8,128)(2,1)} %fusion.47) | data formatting | bytes 25165824 | tf_op jit(solution)/shard_map/convert_element_type | solution.py:55
  719.5 116.1 %reshape.152 = bf16[16,12,2,16384]{3,2,1,0:T(2,128)(2,1)} reshape(bf16[16,12,2,1024,16]{4,3,2,1,0:T(8,128)(2,1)} %copy.153) | data formatting | bytes 25165824 | tf_op jit(solution)/shard_map/convert_element_type | solution.py:55
  (11 shorter events, 0.1 us)
Async XLA Ops:
  104.8 7.0 copy-start.1
  104.8 278.3 %all-to-all-start = ((bf16[16,12,1,16,2,1024]{5,4,3,1,2,0:T(2,128)(2,1)}), bf16[16,12,1,16,2,1024]{5,4,3,1,2,0:T(2,128)(2,1)}, u32[]{:S(2)}, u32[]{:S(2)}) async-start(bf16[16,12,1,16,2,1024]{5,4,3,1,2,0:T(2,128)(2,1)} %fusion.52), calls=%async_computation | async-start | bytes 25165824 | tf_op jit(solution)/shard_map/all_to_all | solution.py:85
  415.2 19.2 %copy-start = (f32[16,16]{1,0:T(8,128)S(1)}, f32[16,16]{1,0:T(8,128)}, u32[]{:S(2)}) copy-start(f32[16,16]{1,0:T(8,128)} %param.11) | copy-start | bytes 3076
  433.1 36.6 %collective-permute-start = (bf16[16,12,2,16,15]{3,0,4,2,1:T(8,128)(2,1)S(1)}, bf16[16,12,2,16,15]{3,0,4,2,1:T(8,128)(2,1)}, u32[]{:S(2)}, u32[]{:S(2)}) collective-permute-start(bf16[16,12,2,16,15]{3,0,4,2,1:T(8,128)(2,1)S(1)} %copy.143), channel_id=1, source_target_pairs={{0,1},{2,3},{4,5},{6,7},{8,9},{10,11},{12,13},{14,15},{16,17},{18,... | collective-permute-start | bytes 552968 | tf_op jit(solution)/shard_map/ppermute | solution.py:11
